TPU v7x, 32 devices: a whole 2x2x4 slice. The times are simulated.
32 devices in a mesh: member: 16 (over z, y, core), slab: 2 (over x).
Axes of the slice: x: 2, y: 2, z: 4, core: 2. Of those that a mesh axis runs over, the one named last changes fastest.
Arguments:
- checkpoint: float32 [16, 2, 4, 256, 256], P('member', None, 'slab'), may hold values from 0 to 1
- adjoint_late: float32 [16, 2, 4, 256, 256], P('member', None, 'slab'), may hold values from -6 to 6
- rate_params: float32 [64, 64], replicated, may hold values from 0.02 to 0.1
- perturbation: float32 [16, 64, 64], P('member'), may hold values from -0.5 to 0.5
Outputs:
- adjoint_early: float32 [16, 2, 4, 256, 256], P('member', None, 'slab')
- param_grad: float32 [64, 64], replicated
All inputs are finite; a program needn't handle non-finite values.
Results may differ from a plain program's by a relative error of at most 0.00002.
Values sent between devices are 32-bit elements; how exact they have to be, the bound alone decides.
A program may use at most 64 MiB of HBM per device.

v0:
```python
import jax
import jax.numpy as jnp
from jax import lax
from jax.sharding import PartitionSpec as P

PX = 64
PY = 64
SX = 4
SY = 4
NX = 256
NY = 256
feed_rate = 0.035
substrate_diffusion = 0.16
activator_diffusion = 0.08


def with_halo(cells, sides, width):
    for axis, dim in sides:
        count = lax.axis_size(axis)
        ends = count - 1
        head = lax.slice_in_dim(cells, 0, width, axis=dim)
        tail = lax.slice_in_dim(cells, cells.shape[dim] - width, cells.shape[dim], axis=dim)
        cells = jnp.concatenate(
            [
                lax.ppermute(tail, axis, [(i, (i + 1) % count) for i in range(ends)]),
                cells,
                lax.ppermute(head, axis, [((i + 1) % count, i) for i in range(ends)]),
            ],
            axis=dim,
        )
    return cells


def laplace_rim(extended):
    padded = jnp.pad(extended, ((0, 0), (0, 0), (1, 1), (1, 1)))
    center = padded[:, 1:-1, 1:-1, 1:-1]
    summed = padded[:, 2:, 1:-1, 1:-1] + padded[:, :-2, 1:-1, 1:-1]
    summed = summed + padded[:, 1:-1, 2:, 1:-1] + padded[:, 1:-1, :-2, 1:-1]
    summed = summed + padded[:, 1:-1, 1:-1, 2:] + padded[:, 1:-1, 1:-1, :-2]
    return summed - 6.0 * center


def advance(extended, decay_rate):
    laplace = laplace_rim(extended)
    u_field = extended[0, 1:-1]
    v_field = extended[1, 1:-1]
    reaction = u_field * v_field * v_field
    u_new = u_field + substrate_diffusion * laplace[0] - reaction + feed_rate * (1.0 - u_field)
    v_new = (
        v_field + activator_diffusion * laplace[1] + reaction - (feed_rate + decay_rate) * v_field
    )
    return jnp.stack([u_new, v_new])


def pull_back(status, adjoint_ext, decay_rate):
    laplace = laplace_rim(adjoint_ext)
    adj_u = adjoint_ext[0, 1:-1]
    adj_v = adjoint_ext[1, 1:-1]
    uv_prod = status[0] * status[1]
    v_square = status[1] * status[1]
    new_u = (
        adj_u + substrate_diffusion * laplace[0] - (v_square + feed_rate) * adj_u + v_square * adj_v
    )
    new_v = (
        adj_v
        + activator_diffusion * laplace[1]
        - 2.0 * uv_prod * adj_u
        + (2.0 * uv_prod - feed_rate - decay_rate) * adj_v
    )
    return jnp.stack([new_u, new_v])


def expand_params(table):
    return jnp.broadcast_to(table[:, None, :, None], (PX, SX, PY, SY)).reshape(NX, NY)


def patch_total(field):
    return jnp.sum(field.reshape(PX, SX, PY, SY), axis=(1, 3))


def local(checkpoint, adjoint_late, rate_params, perturbation):
    start_state = checkpoint[0]
    adjoint_two = adjoint_late[0]
    factor = 1.0 + perturbation[0]
    decay_rate = expand_params(rate_params * factor)
    member_count = lax.axis_size("member")
    state_ext, adjoint_ext_two = (
        with_halo(start_state, (("slab", 1),), 1),
        with_halo(adjoint_two, (("slab", 1),), 1),
    )
    middle = advance(state_ext, decay_rate)
    adjoint_one = pull_back(middle, adjoint_ext_two, decay_rate)
    first_term = -jnp.sum(middle[1] * adjoint_two[1], 0)
    adjoint_ext = with_halo(adjoint_one, (("slab", 1),), 1)
    adjoint_zero = pull_back(start_state, adjoint_ext, decay_rate)
    second = -jnp.sum(start_state[1] * adjoint_one[1], 0)
    param_grad = (
        lax.psum(patch_total(first_term + second) * factor, ("member", "slab")) / member_count
    )
    return (adjoint_zero[None], param_grad)


def solution(mesh):
    return jax.shard_map(
        local,
        mesh=mesh,
        in_specs=(
            P("member", None, "slab", None, None),
            P("member", None, "slab", None, None),
            P(),
            P("member", None, None),
        ),
        out_specs=(P("member", None, "slab", None, None), P()),
        check_vma=False,
    )
```

profile of v0, /device:TPU:0, one launch (start us, length us, event | category | flops | bytes accessed | tf_op | source)
XLA Modules:
  0.0 109.7 jit_solution(6081477376851431871)
XLA Ops:
  0.6 0.0 copy-start.5
  0.6 0.0 copy-start.4
  0.6 2.3 %fusion.44 = (f32[2,1,256,256]{3,2,1,0:T(8,128)}, f32[2,1,256,256]{3,2,1,0:T(8,128)}) fusion(f32[2,2,256,256]{3,2,1,0:T(8,128)} %bitcast.149), kind=kLoop, calls=%fused_computation.112 | loop fusion | bytes 2097152 | tf_op jit(solution)/shard_map/slice | solution.py:22
  2.9 1.3 %collective-permute-start = (f32[2,1,256,256]{3,2,1,0:T(8,128)}, f32[2,1,256,256]{3,2,1,0:T(8,128)S(1)}, u32[]{:S(2)}, u32[]{:S(2)}) collective-permute-start(f32[2,1,256,256]{3,2,1,0:T(8,128)} %get-tuple-element.13), channel_id=1, source_target_pairs={{1,0},{3,2},{5,4},{7,6},{9,8},{11,10},{13,12},{15,14},{17,16},{19,... | collective-permute-start | bytes 1572872 | tf_op jit(solution)/shard_map/ppermute | solution.py:27
  4.2 4.9 %collective-permute-start.1 = (f32[2,1,256,256]{3,2,1,0:T(8,128)}, f32[2,1,256,256]{3,2,1,0:T(8,128)S(1)}, u32[]{:S(2)}, u32[]{:S(2)}) collective-permute-start(f32[2,1,256,256]{3,2,1,0:T(8,128)} %get-tuple-element.12), channel_id=1, source_target_pairs={{0,1},{2,3},{4,5},{6,7},{8,9},{10,11},{12,13},{14,15},{16,17},{18,... | collective-permute-start | bytes 1572872 | tf_op jit(solution)/shard_map/ppermute | solution.py:25
  9.1 2.4 %fusion.43 = (f32[2,1,256,256]{3,2,1,0:T(8,128)}, f32[2,1,256,256]{3,2,1,0:T(8,128)}) fusion(f32[2,2,256,256]{3,2,1,0:T(8,128)} %bitcast.146), kind=kLoop, calls=%fused_computation.111 | loop fusion | bytes 2097152 | tf_op jit(solution)/shard_map/slice | solution.py:22
  11.5 1.3 %collective-permute-start.2 = (f32[2,1,256,256]{3,2,1,0:T(8,128)}, f32[2,1,256,256]{3,2,1,0:T(8,128)S(1)}, u32[]{:S(2)}, u32[]{:S(2)}) collective-permute-start(f32[2,1,256,256]{3,2,1,0:T(8,128)} %get-tuple-element.11), channel_id=1, source_target_pairs={{1,0},{3,2},{5,4},{7,6},{9,8},{11,10},{13,12},{15,14},{17,16},{19,... | collective-permute-start | bytes 1572872 | tf_op jit(solution)/shard_map/ppermute | solution.py:27
  12.8 5.4 %collective-permute-start.3 = (f32[2,1,256,256]{3,2,1,0:T(8,128)}, f32[2,1,256,256]{3,2,1,0:T(8,128)}, u32[]{:S(2)}, u32[]{:S(2)}) collective-permute-start(f32[2,1,256,256]{3,2,1,0:T(8,128)} %get-tuple-element.10), channel_id=1, source_target_pairs={{0,1},{2,3},{4,5},{6,7},{8,9},{10,11},{12,13},{14,15},{16,17},{18,... | collective-permute-start | bytes 1572872 | tf_op jit(solution)/shard_map/ppermute | solution.py:25
  18.2 0.0 copy-done.5
  18.2 0.0 copy-done.4
  18.2 3.8 %broadcast_in_dim.4 = f32[64,4,64,4]{3,2,1,0:T(8,128)} broadcast(f32[64,64]{1,0:T(8,128)S(1)} %bitcast_multiply_fusion.13), dimensions={0,2} | broadcast | bytes 278528 | tf_op jit(solution)/shard_map/broadcast_in_dim | solution.py:74
  22.0 0.0 copy-start.1
  22.0 8.4 %reshape.133 = f32[256,256]{1,0:T(8,128)S(1)} reshape(f32[64,4,64,4]{3,2,1,0:T(8,128)} %broadcast_in_dim.4) | data formatting | bytes 524288 | tf_op jit(solution)/shard_map/reshape | solution.py:74
  30.4 0.0 collective-permute-done
  30.4 0.0 copy-start.2
  30.4 0.0 collective-permute-done.1
  30.5 0.8 copy-done.2
  31.2 0.0 copy-start.3
  31.2 0.8 copy-done.3
  32.0 0.0 copy-done.1
  32.0 1.4 %select_maximum_fusion.5 = f32[2,4,258,258]{3,2,1,0:T(8,128)S(1)} fusion(f32[2,1,256,256]{3,2,1,0:T(8,128)S(1)} %collective-permute-done, f32[2,2,256,256]{3,2,1,0:T(8,128)S(1)} %bitcast.150, f32[2,1,256,256]{3,2,1,0:T(8,128)S(1)} %collective-permute-done.1), kind=kLoop, calls=%fused_computation.9 | loop fusion | flops 7987680 | bytes 4227200 | tf_op jit(solution)/shard_map/concatenate | solution.py:23
  33.5 0.0 copy-start
  33.5 2.2 %fusion.8 = f32[2,2,256,256]{3,2,1,0:T(8,128)S(1)} fusion(f32[2,4,258,258]{3,2,1,0:T(8,128)S(1)} %select_maximum_fusion.5, f32[2,2,256,256]{3,2,1,0:T(8,128)S(1)} %bitcast.151, f32[2,1,256,256]{3,2,1,0:T(8,128)} %copy-done.3, f32[2,1,256,256]{3,2,1,0:T(8,128)} %copy-done.2), kind=kLoop, calls=%fused_computation.39 | loop fusion | flops 2359296 | bytes 7340032 | tf_op jit(solution)/shard_map/sub | solution.py:40
  35.7 0.0 collective-permute-done.2
  35.7 0.0 collective-permute-done.3
  35.7 0.0 copy-done
  35.7 2.4 %select_maximum_fusion.3 = f32[2,4,258,258]{3,2,1,0:T(8,128)S(1)} fusion(f32[2,1,256,256]{3,2,1,0:T(8,128)S(1)} %collective-permute-done.2, f32[2,2,256,256]{3,2,1,0:T(8,128)S(1)} %bitcast.147, f32[2,1,256,256]{3,2,1,0:T(8,128)} %collective-permute-done.3), kind=kLoop, calls=%fused_computation.7 | loop fusion | flops 7987680 | bytes 4227200 | tf_op jit(solution)/shard_map/concatenate | solution.py:23
  38.2 2.0 %fusion.6 = f32[2,2,256,256]{3,2,1,0:T(8,128)S(1)} fusion(f32[2,4,258,258]{3,2,1,0:T(8,128)S(1)} %select_maximum_fusion.3, f32[2,2,256,256]{3,2,1,0:T(8,128)S(1)} %bitcast.148, f32[2,1,256,256]{3,2,1,0:T(8,128)} %collective-permute-done.3, f32[2,1,256,256]{3,2,1,0:T(8,128)S(1)} %collective-permute-done.2), kind=kLoop, calls=%fused_computation.31 | loop fusion | flops 2359296 | bytes 7340032 | tf_op jit(solution)/shard_map/sub | solution.py:40
  40.2 0.3 fusion.20
  40.4 0.5 fusion.29
  40.9 0.4 fusion.34
  41.3 1.1 fusion.11
  42.4 1.3 %collective-permute-start.4 = (f32[2,1,256,256]{3,2,1,0:T(8,128)}, f32[2,1,256,256]{3,2,1,0:T(8,128)S(1)}, u32[]{:S(2)}, u32[]{:S(2)}) collective-permute-start(f32[2,1,256,256]{3,2,1,0:T(8,128)} %get-tuple-element.9), channel_id=1, source_target_pairs={{1,0},{3,2},{5,4},{7,6},{9,8},{11,10},{13,12},{15,14},{17,16},{19,... | collective-permute-start | bytes 1572872 | tf_op jit(solution)/shard_map/ppermute | solution.py:27
  43.7 4.6 %collective-permute-start.5 = (f32[2,1,256,256]{3,2,1,0:T(8,128)}, f32[2,1,256,256]{3,2,1,0:T(8,128)S(1)}, u32[]{:S(2)}, u32[]{:S(2)}) collective-permute-start(f32[2,1,256,256]{3,2,1,0:T(8,128)} %get-tuple-element.8), channel_id=1, source_target_pairs={{0,1},{2,3},{4,5},{6,7},{8,9},{10,11},{12,13},{14,15},{16,17},{18,... | collective-permute-start | bytes 1572872 | tf_op jit(solution)/shard_map/ppermute | solution.py:25
  48.3 0.8 negate_add_fusion
  49.0 10.8 %add.226 = f32[64,4,64,4]{3,2,1,0:T(8,128)} reshape(f32[256,256]{1,0:T(8,128)} %negate_add_fusion) | data formatting | bytes 524288 | tf_op jit(solution)/shard_map/add | solution.py:98
  59.9 4.0 %reduce_sum.29 = f32[64,64]{1,0:T(8,128)S(1)} reduce(f32[64,4,64,4]{3,2,1,0:T(8,128)} %add.226, f32[]{:T(128)} %constant.9.clone.1), dimensions={1,3}, to_apply=%region_2.3 | reduce | flops 61440 | bytes 278532 | tf_op jit(solution)/shard_map/reduce_sum | solution.py:78
  63.9 41.0 %psum.7 = f32[64,64]{1,0:T(8,128)S(1)} all-reduce(f32[64,64]{1,0:T(8,128)S(1)} %bitcast_multiply_fusion.12), channel_id=1, replica_groups=mesh['member'=16,'slab'=2] {'member','slab'}, use_global_device_ids=true, to_apply=%region_3.4 | all-reduce | flops 4096 | bytes 32768 | tf_op jit(solution)/shard_map/psum | solution.py:98
  104.9 0.6 broadcast_multiply_fusion
  105.5 0.0 collective-permute-done.4
  105.5 0.0 collective-permute-done.5
  105.5 1.9 %select_maximum_fusion = f32[2,4,258,258]{3,2,1,0:T(8,128)S(1)} fusion(f32[2,1,256,256]{3,2,1,0:T(8,128)S(1)} %collective-permute-done.4, f32[2,1,256,256]{3,2,1,0:T(8,128)S(1)} %collective-permute-done.5, f32[1,2,256,256]{3,2,1,0:T(8,128)S(1)} %fusion.34, f32[1,2,256,256]{3,2,1,0:T(8,128)S(1)} %get-tuple-element.4), kind=kLoop, calls=%fused_computation.4 | loop fusion | flops 9585216 | bytes 4227200 | tf_op jit(solution)/shard_map/concatenate | solution.py:23
  107.4 0.9 fusion.4
  108.4 0.3 fusion.17
  108.7 1.0 maximum_bitcast_fusion
  (3 shorter events, 0.0 us)
Async XLA Ops:
  0.6 17.5 %copy-start.5 = (f32[64,64]{1,0:T(8,128)S(1)}, f32[64,64]{1,0:T(8,128)}, u32[]{:S(2)}) copy-start(f32[64,64]{1,0:T(8,128)} %param.6) | copy-start | bytes 49156
  0.6 17.5 %copy-start.4 = (f32[1,64,64]{2,1,0:T(8,128)S(1)}, f32[1,64,64]{2,1,0:T(8,128)}, u32[]{:S(2)}) copy-start(f32[1,64,64]{2,1,0:T(8,128)} %param.7) | copy-start | bytes 49156
  2.9 27.5 %collective-permute-start = (f32[2,1,256,256]{3,2,1,0:T(8,128)}, f32[2,1,256,256]{3,2,1,0:T(8,128)S(1)}, u32[]{:S(2)}, u32[]{:S(2)}) collective-permute-start(f32[2,1,256,256]{3,2,1,0:T(8,128)} %get-tuple-element.13), channel_id=1, source_target_pairs={{1,0},{3,2},{5,4},{7,6},{9,8},{11,10},{13,12},{15,14},{17,16},{19,... | collective-permute-start | bytes 1572872 | tf_op jit(solution)/shard_map/ppermute | solution.py:27
  4.2 26.3 %collective-permute-start.1 = (f32[2,1,256,256]{3,2,1,0:T(8,128)}, f32[2,1,256,256]{3,2,1,0:T(8,128)S(1)}, u32[]{:S(2)}, u32[]{:S(2)}) collective-permute-start(f32[2,1,256,256]{3,2,1,0:T(8,128)} %get-tuple-element.12), channel_id=1, source_target_pairs={{0,1},{2,3},{4,5},{6,7},{8,9},{10,11},{12,13},{14,15},{16,17},{18,... | collective-permute-start | bytes 1572872 | tf_op jit(solution)/shard_map/ppermute | solution.py:25
  11.5 24.2 %collective-permute-start.2 = (f32[2,1,256,256]{3,2,1,0:T(8,128)}, f32[2,1,256,256]{3,2,1,0:T(8,128)S(1)}, u32[]{:S(2)}, u32[]{:S(2)}) collective-permute-start(f32[2,1,256,256]{3,2,1,0:T(8,128)} %get-tuple-element.11), channel_id=1, source_target_pairs={{1,0},{3,2},{5,4},{7,6},{9,8},{11,10},{13,12},{15,14},{17,16},{19,... | collective-permute-start | bytes 1572872 | tf_op jit(solution)/shard_map/ppermute | solution.py:27
  12.8 23.0 %collective-permute-start.3 = (f32[2,1,256,256]{3,2,1,0:T(8,128)}, f32[2,1,256,256]{3,2,1,0:T(8,128)}, u32[]{:S(2)}, u32[]{:S(2)}) collective-permute-start(f32[2,1,256,256]{3,2,1,0:T(8,128)} %get-tuple-element.10), channel_id=1, source_target_pairs={{0,1},{2,3},{4,5},{6,7},{8,9},{10,11},{12,13},{14,15},{16,17},{18,... | collective-permute-start | bytes 1572872 | tf_op jit(solution)/shard_map/ppermute | solution.py:25
  22.0 10.0 %copy-start.1 = (f32[1,2,2,256,256]{4,3,2,1,0:T(8,128)S(1)}, f32[1,2,2,256,256]{4,3,2,1,0:T(8,128)}, u32[]{:S(2)}) copy-start(f32[1,2,2,256,256]{4,3,2,1,0:T(8,128)} %param.5) | copy-start | bytes 3145732
  30.4 0.8 copy-start.2
  31.2 0.8 copy-start.3
  33.5 2.3 %copy-start = (f32[1,2,2,256,256]{4,3,2,1,0:T(8,128)S(1)}, f32[1,2,2,256,256]{4,3,2,1,0:T(8,128)}, u32[]{:S(2)}) copy-start(f32[1,2,2,256,256]{4,3,2,1,0:T(8,128)} %param.4) | copy-start | bytes 3145732
  42.4 63.2 %collective-permute-start.4 = (f32[2,1,256,256]{3,2,1,0:T(8,128)}, f32[2,1,256,256]{3,2,1,0:T(8,128)S(1)}, u32[]{:S(2)}, u32[]{:S(2)}) collective-permute-start(f32[2,1,256,256]{3,2,1,0:T(8,128)} %get-tuple-element.9), channel_id=1, source_target_pairs={{1,0},{3,2},{5,4},{7,6},{9,8},{11,10},{13,12},{15,14},{17,16},{19,... | collective-permute-start | bytes 1572872 | tf_op jit(solution)/shard_map/ppermute | solution.py:27
  43.7 61.9 %collective-permute-start.5 = (f32[2,1,256,256]{3,2,1,0:T(8,128)}, f32[2,1,256,256]{3,2,1,0:T(8,128)S(1)}, u32[]{:S(2)}, u32[]{:S(2)}) collective-permute-start(f32[2,1,256,256]{3,2,1,0:T(8,128)} %get-tuple-element.8), channel_id=1, source_target_pairs={{0,1},{2,3},{4,5},{6,7},{8,9},{10,11},{12,13},{14,15},{16,17},{18,... | collective-permute-start | bytes 1572872 | tf_op jit(solution)/shard_map/ppermute | solution.py:25
where the time goes:
time: 110 us
  blocking collectives  41 us (37%)
  local copies, waits for them, and re-layouts  29.3 us (27%)
  other arithmetic  19.8 us (18%)
  starting transfers between devices  18.8 us (17%)
    psum x1, blocking collectives, local(): lax.psum(patch_total(first_term + second) * factor, ('member', 'slab'))  41 us
    ppermute x3, starting transfers between devices, with_halo(): lax.ppermute(tail, axis, [(i, (i + 1) % count) for i in range(ends)])  14.9 us
    add x1, local copies, waits for them, and re-layouts, local(): first_term + second  10.8 us
    reshape x1, local copies, waits for them, and re-layouts, expand_params(): jnp.broadcast_to(table[:, None, :, None], (PX, SX, PY, SY)).reshape(NX, NY)  8.39 us
    concatenate x3, other arithmetic, with_halo(): jnp.concatenate([lax.ppermute(tail, axis, [(i, (i + 1) % count) for i in...  5.74 us
    sub x3, other arithmetic, laplace_rim(): return summed - 6.0 * center  5.14 us
    slice x2, local copies, waits for them, and re-layouts, with_halo(): lax.slice_in_dim(cells, cells.shape[dim] - width, cells.shape[dim], axis=...  4.61 us
    reduce_sum x1, other arithmetic, patch_total(): return jnp.sum(field.reshape(PX, SX, PY, SY), axis=(1, 3))  4.01 us
  transfers between devices with their start and end apart: 6, of which 0 were waited for; matrix products, arithmetic and copies ran while one was open for 31% of the time, Pallas kernels for 0%

commit v1 on v0

--- a/solution.py
+++ b/solution.py
@@ -2,6 +2,7 @@
 import jax.numpy as jnp
 from jax import lax
 from jax.sharding import PartitionSpec as P
+from jax.lax import psum
 
 PX = 64
 PY = 64
@@ -94,8 +95,13 @@
     adjoint_ext = with_halo(adjoint_one, (("slab", 1),), 1)
     adjoint_zero = pull_back(start_state, adjoint_ext, decay_rate)
     second = -jnp.sum(start_state[1] * adjoint_one[1], 0)
+
+    def _pair_page(chunk, link_axis, comm_axis):
+        return psum(psum(chunk, link_axis), comm_axis)
+
     param_grad = (
-        lax.psum(patch_total(first_term + second) * factor, ("member", "slab")) / member_count
+        _pair_page(patch_total(first_term + second) * factor, link_axis="slab", comm_axis="member")
+        / member_count
     )
     return (adjoint_zero[None], param_grad)
 

time: 110 us -> 135 us (1.23)
  blocking collectives: 41 us -> 66.1 us
    psum x1 -> x2, blocking collectives: 41 us -> 66.1 us  [_pair_page(): return psum(psum(chunk, link_axis), comm_axis)]
  transfers between devices with their start and end apart: 6 -> 6, of which waited for: 0 -> 0; matrix products, arithmetic and copies ran while one was open for 31% -> 26% of each run, Pallas kernels for 0% -> 0%
where the time goes in v1:
time: 135 us
  blocking collectives  66.1 us (49%)
  local copies, waits for them, and re-layouts  29.2 us (22%)
  other arithmetic  19.8 us (15%)
  starting transfers between devices  18.7 us (14%)
    psum x2, blocking collectives, _pair_page(): return psum(psum(chunk, link_axis), comm_axis)  66.1 us
    ppermute x3, starting transfers between devices, with_halo(): lax.ppermute(tail, axis, [(i, (i + 1) % count) for i in range(ends)])  14.9 us
    add x1, local copies, waits for them, and re-layouts, local(): first_term + second  10.8 us
    reshape x1, local copies, waits for them, and re-layouts, expand_params(): jnp.broadcast_to(table[:, None, :, None], (PX, SX, PY, SY)).reshape(NX, NY)  8.39 us
    concatenate x3, other arithmetic, with_halo(): jnp.concatenate([lax.ppermute(tail, axis, [(i, (i + 1) % count) for i in...  5.74 us
    sub x3, other arithmetic, laplace_rim(): return summed - 6.0 * center  5.14 us
    slice x2, local copies, waits for them, and re-layouts, with_halo(): lax.slice_in_dim(cells, cells.shape[dim] - width, cells.shape[dim], axis=...  4.61 us
    reduce_sum x1, other arithmetic, patch_total(): return jnp.sum(field.reshape(PX, SX, PY, SY), axis=(1, 3))  4.01 us
  transfers between devices with their start and end apart: 6, of which 0 were waited for; matrix products, arithmetic and copies ran while one was open for 26% of the time, Pallas kernels for 0%

profile of v1, /device:TPU:0, one launch (start us, length us, event | category | flops | bytes accessed | tf_op | source)
XLA Modules:
  0.0 134.8 jit_solution(4622831404279492078)
XLA Ops:
  0.6 0.0 copy-start.5
  0.6 0.0 copy-start.4
  0.6 2.3 %fusion.44 = (f32[2,1,256,256]{3,2,1,0:T(8,128)}, f32[2,1,256,256]{3,2,1,0:T(8,128)}) fusion(f32[2,2,256,256]{3,2,1,0:T(8,128)} %bitcast.149), kind=kLoop, calls=%fused_computation.112 | loop fusion | bytes 2097152 | tf_op jit(solution)/shard_map/slice | solution.py:23
  2.9 1.3 collective-permute-start
  4.2 4.9 %collective-permute-start.1 = (f32[2,1,256,256]{3,2,1,0:T(8,128)}, f32[2,1,256,256]{3,2,1,0:T(8,128)S(1)}, u32[]{:S(2)}, u32[]{:S(2)}) collective-permute-start(f32[2,1,256,256]{3,2,1,0:T(8,128)} %get-tuple-element.12), channel_id=1, source_target_pairs={{0,1},{2,3},{4,5},{6,7},{8,9},{10,11},{12,13},{14,15},{16,17},{18,... | collective-permute-start | bytes 1572872 | tf_op jit(solution)/shard_map/ppermute | solution.py:26
  9.1 2.4 %fusion.43 = (f32[2,1,256,256]{3,2,1,0:T(8,128)}, f32[2,1,256,256]{3,2,1,0:T(8,128)}) fusion(f32[2,2,256,256]{3,2,1,0:T(8,128)} %bitcast.146), kind=kLoop, calls=%fused_computation.111 | loop fusion | bytes 2097152 | tf_op jit(solution)/shard_map/slice | solution.py:23
  11.5 1.3 collective-permute-start.2
  12.8 5.4 %collective-permute-start.3 = (f32[2,1,256,256]{3,2,1,0:T(8,128)}, f32[2,1,256,256]{3,2,1,0:T(8,128)}, u32[]{:S(2)}, u32[]{:S(2)}) collective-permute-start(f32[2,1,256,256]{3,2,1,0:T(8,128)} %get-tuple-element.10), channel_id=1, source_target_pairs={{0,1},{2,3},{4,5},{6,7},{8,9},{10,11},{12,13},{14,15},{16,17},{18,... | collective-permute-start | bytes 1572872 | tf_op jit(solution)/shard_map/ppermute | solution.py:26
  18.1 0.0 copy-done.5
  18.1 0.0 copy-done.4
  18.2 3.8 %broadcast_in_dim.4 = f32[64,4,64,4]{3,2,1,0:T(8,128)} broadcast(f32[64,64]{1,0:T(8,128)S(1)} %bitcast_multiply_fusion.13), dimensions={0,2} | broadcast | bytes 278528 | tf_op jit(solution)/shard_map/broadcast_in_dim | solution.py:75
  22.0 0.0 copy-start.1
  22.0 8.4 %reshape.133 = f32[256,256]{1,0:T(8,128)S(1)} reshape(f32[64,4,64,4]{3,2,1,0:T(8,128)} %broadcast_in_dim.4) | data formatting | bytes 524288 | tf_op jit(solution)/shard_map/reshape | solution.py:75
  30.4 0.0 collective-permute-done
  30.4 0.0 copy-start.2
  30.4 0.0 collective-permute-done.1
  30.4 0.8 copy-done.2
  31.2 0.0 copy-start.3
  31.2 0.8 copy-done.3
  32.0 0.0 copy-done.1
  32.0 1.4 %select_maximum_fusion.5 = f32[2,4,258,258]{3,2,1,0:T(8,128)S(1)} fusion(f32[2,1,256,256]{3,2,1,0:T(8,128)S(1)} %collective-permute-done, f32[2,2,256,256]{3,2,1,0:T(8,128)S(1)} %bitcast.150, f32[2,1,256,256]{3,2,1,0:T(8,128)S(1)} %collective-permute-done.1), kind=kLoop, calls=%fused_computation.9 | loop fusion | flops 7987680 | bytes 4227200 | tf_op jit(solution)/shard_map/concatenate | solution.py:24
  33.5 0.0 copy-start
  33.5 2.2 %fusion.8 = f32[2,2,256,256]{3,2,1,0:T(8,128)S(1)} fusion(f32[2,4,258,258]{3,2,1,0:T(8,128)S(1)} %select_maximum_fusion.5, f32[2,2,256,256]{3,2,1,0:T(8,128)S(1)} %bitcast.151, f32[2,1,256,256]{3,2,1,0:T(8,128)} %copy-done.3, f32[2,1,256,256]{3,2,1,0:T(8,128)} %copy-done.2), kind=kLoop, calls=%fused_computation.39 | loop fusion | flops 2359296 | bytes 7340032 | tf_op jit(solution)/shard_map/sub | solution.py:41
  35.7 0.0 collective-permute-done.2
  35.7 0.0 collective-permute-done.3
  35.7 0.0 copy-done
  35.7 2.4 %select_maximum_fusion.3 = f32[2,4,258,258]{3,2,1,0:T(8,128)S(1)} fusion(f32[2,1,256,256]{3,2,1,0:T(8,128)S(1)} %collective-permute-done.2, f32[2,2,256,256]{3,2,1,0:T(8,128)S(1)} %bitcast.147, f32[2,1,256,256]{3,2,1,0:T(8,128)} %collective-permute-done.3), kind=kLoop, calls=%fused_computation.7 | loop fusion | flops 7987680 | bytes 4227200 | tf_op jit(solution)/shard_map/concatenate | solution.py:24
  38.2 2.0 %fusion.6 = f32[2,2,256,256]{3,2,1,0:T(8,128)S(1)} fusion(f32[2,4,258,258]{3,2,1,0:T(8,128)S(1)} %select_maximum_fusion.3, f32[2,2,256,256]{3,2,1,0:T(8,128)S(1)} %bitcast.148, f32[2,1,256,256]{3,2,1,0:T(8,128)} %collective-permute-done.3, f32[2,1,256,256]{3,2,1,0:T(8,128)S(1)} %collective-permute-done.2), kind=kLoop, calls=%fused_computation.31 | loop fusion | flops 2359296 | bytes 7340032 | tf_op jit(solution)/shard_map/sub | solution.py:41
  40.2 0.3 fusion.20
  40.4 0.5 fusion.29
  40.9 0.4 fusion.34
  41.3 1.1 fusion.11
  42.3 1.3 collective-permute-start.4
  43.6 4.6 %collective-permute-start.5 = (f32[2,1,256,256]{3,2,1,0:T(8,128)}, f32[2,1,256,256]{3,2,1,0:T(8,128)S(1)}, u32[]{:S(2)}, u32[]{:S(2)}) collective-permute-start(f32[2,1,256,256]{3,2,1,0:T(8,128)} %get-tuple-element.8), channel_id=1, source_target_pairs={{0,1},{2,3},{4,5},{6,7},{8,9},{10,11},{12,13},{14,15},{16,17},{18,... | collective-permute-start | bytes 1572872 | tf_op jit(solution)/shard_map/ppermute | solution.py:26
  48.3 0.8 negate_add_fusion
  49.0 10.8 %add.228 = f32[64,4,64,4]{3,2,1,0:T(8,128)} reshape(f32[256,256]{1,0:T(8,128)} %negate_add_fusion) | data formatting | bytes 524288 | tf_op jit(solution)/shard_map/add | solution.py:103
  59.8 4.0 %reduce_sum.29 = f32[64,64]{1,0:T(8,128)S(1)} reduce(f32[64,4,64,4]{3,2,1,0:T(8,128)} %add.228, f32[]{:T(128)} %constant.9.clone.1), dimensions={1,3}, to_apply=%region_2.3 | reduce | flops 61440 | bytes 278532 | tf_op jit(solution)/shard_map/reduce_sum | solution.py:79
  63.9 6.9 %psum.14 = f32[64,64]{1,0:T(8,128)S(1)} all-reduce(f32[64,64]{1,0:T(8,128)S(1)} %bitcast_multiply_fusion.12), channel_id=1, replica_groups=mesh['member'=16,'slab'=2] {'slab'}, use_global_device_ids=true, to_apply=%region_3.4 | all-reduce | flops 4096 | bytes 32768 | tf_op jit(solution)/shard_map/psum | solution.py:100
  70.8 59.2 %psum.15 = f32[64,64]{1,0:T(8,128)S(1)} all-reduce(f32[64,64]{1,0:T(8,128)S(1)} %psum.14), channel_id=1, replica_groups=mesh['member'=16,'slab'=2] {'member'}, use_global_device_ids=true, to_apply=%region_4.5 | all-reduce | flops 4096 | bytes 32768 | tf_op jit(solution)/shard_map/psum | solution.py:100
  130.0 0.6 broadcast_multiply_fusion
  130.6 0.0 collective-permute-done.4
  130.6 0.0 collective-permute-done.5
  130.6 1.9 %select_maximum_fusion = f32[2,4,258,258]{3,2,1,0:T(8,128)S(1)} fusion(f32[2,1,256,256]{3,2,1,0:T(8,128)S(1)} %collective-permute-done.4, f32[2,1,256,256]{3,2,1,0:T(8,128)S(1)} %collective-permute-done.5, f32[1,2,256,256]{3,2,1,0:T(8,128)S(1)} %fusion.34, f32[1,2,256,256]{3,2,1,0:T(8,128)S(1)} %get-tuple-element.4), kind=kLoop, calls=%fused_computation.4 | loop fusion | flops 9585216 | bytes 4227200 | tf_op jit(solution)/shard_map/concatenate | solution.py:24
  132.5 0.9 fusion.4
  133.5 0.3 fusion.17
  133.8 1.0 maximum_bitcast_fusion
  (3 shorter events, 0.0 us)
Async XLA Ops:
  0.6 17.5 %copy-start.5 = (f32[64,64]{1,0:T(8,128)S(1)}, f32[64,64]{1,0:T(8,128)}, u32[]{:S(2)}) copy-start(f32[64,64]{1,0:T(8,128)} %param.6) | copy-start | bytes 49156
  0.6 17.5 %copy-start.4 = (f32[1,64,64]{2,1,0:T(8,128)S(1)}, f32[1,64,64]{2,1,0:T(8,128)}, u32[]{:S(2)}) copy-start(f32[1,64,64]{2,1,0:T(8,128)} %param.7) | copy-start | bytes 49156
  2.9 27.5 %collective-permute-start = (f32[2,1,256,256]{3,2,1,0:T(8,128)}, f32[2,1,256,256]{3,2,1,0:T(8,128)S(1)}, u32[]{:S(2)}, u32[]{:S(2)}) collective-permute-start(f32[2,1,256,256]{3,2,1,0:T(8,128)} %get-tuple-element.13), channel_id=1, source_target_pairs={{1,0},{3,2},{5,4},{7,6},{9,8},{11,10},{13,12},{15,14},{17,16},{19,... | collective-permute-start | bytes 1572872 | tf_op jit(solution)/shard_map/ppermute | solution.py:28
  4.2 26.2 %collective-permute-start.1 = (f32[2,1,256,256]{3,2,1,0:T(8,128)}, f32[2,1,256,256]{3,2,1,0:T(8,128)S(1)}, u32[]{:S(2)}, u32[]{:S(2)}) collective-permute-start(f32[2,1,256,256]{3,2,1,0:T(8,128)} %get-tuple-element.12), channel_id=1, source_target_pairs={{0,1},{2,3},{4,5},{6,7},{8,9},{10,11},{12,13},{14,15},{16,17},{18,... | collective-permute-start | bytes 1572872 | tf_op jit(solution)/shard_map/ppermute | solution.py:26
  11.5 24.2 %collective-permute-start.2 = (f32[2,1,256,256]{3,2,1,0:T(8,128)}, f32[2,1,256,256]{3,2,1,0:T(8,128)S(1)}, u32[]{:S(2)}, u32[]{:S(2)}) collective-permute-start(f32[2,1,256,256]{3,2,1,0:T(8,128)} %get-tuple-element.11), channel_id=1, source_target_pairs={{1,0},{3,2},{5,4},{7,6},{9,8},{11,10},{13,12},{15,14},{17,16},{19,... | collective-permute-start | bytes 1572872 | tf_op jit(solution)/shard_map/ppermute | solution.py:28
  12.8 22.9 %collective-permute-start.3 = (f32[2,1,256,256]{3,2,1,0:T(8,128)}, f32[2,1,256,256]{3,2,1,0:T(8,128)}, u32[]{:S(2)}, u32[]{:S(2)}) collective-permute-start(f32[2,1,256,256]{3,2,1,0:T(8,128)} %get-tuple-element.10), channel_id=1, source_target_pairs={{0,1},{2,3},{4,5},{6,7},{8,9},{10,11},{12,13},{14,15},{16,17},{18,... | collective-permute-start | bytes 1572872 | tf_op jit(solution)/shard_map/ppermute | solution.py:26
  22.0 10.0 %copy-start.1 = (f32[1,2,2,256,256]{4,3,2,1,0:T(8,128)S(1)}, f32[1,2,2,256,256]{4,3,2,1,0:T(8,128)}, u32[]{:S(2)}) copy-start(f32[1,2,2,256,256]{4,3,2,1,0:T(8,128)} %param.5) | copy-start | bytes 3145732
  30.4 0.8 copy-start.2
  31.2 0.8 copy-start.3
  33.5 2.3 %copy-start = (f32[1,2,2,256,256]{4,3,2,1,0:T(8,128)S(1)}, f32[1,2,2,256,256]{4,3,2,1,0:T(8,128)}, u32[]{:S(2)}) copy-start(f32[1,2,2,256,256]{4,3,2,1,0:T(8,128)} %param.4) | copy-start | bytes 3145732
  42.3 88.3 %collective-permute-start.4 = (f32[2,1,256,256]{3,2,1,0:T(8,128)}, f32[2,1,256,256]{3,2,1,0:T(8,128)S(1)}, u32[]{:S(2)}, u32[]{:S(2)}) collective-permute-start(f32[2,1,256,256]{3,2,1,0:T(8,128)} %get-tuple-element.9), channel_id=1, source_target_pairs={{1,0},{3,2},{5,4},{7,6},{9,8},{11,10},{13,12},{15,14},{17,16},{19,... | collective-permute-start | bytes 1572872 | tf_op jit(solution)/shard_map/ppermute | solution.py:28
  43.6 87.0 %collective-permute-start.5 = (f32[2,1,256,256]{3,2,1,0:T(8,128)}, f32[2,1,256,256]{3,2,1,0:T(8,128)S(1)}, u32[]{:S(2)}, u32[]{:S(2)}) collective-permute-start(f32[2,1,256,256]{3,2,1,0:T(8,128)} %get-tuple-element.8), channel_id=1, source_target_pairs={{0,1},{2,3},{4,5},{6,7},{8,9},{10,11},{12,13},{14,15},{16,17},{18,... | collective-permute-start | bytes 1572872 | tf_op jit(solution)/shard_map/ppermute | solution.py:26
